TPU v7x, 32 devices: a whole 2x2x4 slice. The times are simulated.
32 devices in a mesh: dp: 8 (over z, x), fsdp: 4 (over y, core).
Axes of the slice: x: 2, y: 2, z: 4, core: 2. Of those that a mesh axis runs over, the one named last changes fastest.
Arguments:
- patches: bfloat16 [8, 4, 192, 64], P('dp', 'fsdp'), may hold values from -6 to 6
- noise: bfloat16 [8, 4, 192, 64], P('dp', 'fsdp'), may hold values from -6 to 6
- bucket: int32 [8, 4], P(None, 'fsdp'), may hold values from 0 to 11
- tstep: int32 [8, 4], P('dp', 'fsdp'), may hold values from 0 to 999
- dest: int32 [8, 4], P(None, 'fsdp'), may hold values from 0 to 7, as said below
- embed_weight: bfloat16 [64, 2432], replicated, may hold values from -0.75 to 0.75
- gain: float32 [2432], replicated, may hold values from 0.1 to 1.9
- proj_weight: bfloat16 [2432, 1216], P('fsdp'), may hold values from -0.125 to 0.125
- cotangent: bfloat16 [8, 4, 2, 192, 1216], P('dp', 'fsdp'), may hold values from -6 to 6
Outputs:
- projected: bfloat16 [8, 4, 2, 192, 1216], P('dp', 'fsdp')
- embed_grad: float32 [64, 2432], replicated
Inputs may be any that keep to these rules, and one draw needn't show every extreme that they name: `dest`: in every column f, each dp index is named by at most 2 images and by exactly 2 for some.
All inputs are finite; a program needn't handle non-finite values.
Results may differ from a plain program's by a relative error of at most 0.006.
Values may be sent and summed in bfloat16 or wider, within the bound.
A program may use at most 64 MiB of HBM per device.

v0:
```python
import jax
import jax.numpy as jnp
from jax import lax
from jax.sharding import PartitionSpec as P

TOK_MAX = 192
CAP = 2
BUCKETS = 12
TSTEPS = 1000
norm_eps = 1e-06


def lengths_of(bucket):
    stride = max(1, TOK_MAX // (2 * BUCKETS))
    return TOK_MAX - bucket * stride


def noise_level(tstep, length):
    frac = (tstep.astype(jnp.float32) + 1.0) / TSTEPS
    shift = 1.0 + 2.0 * length.astype(jnp.float32) / TOK_MAX
    return shift * frac / (1.0 + (shift - 1.0) * frac)


def body(patches, noise, bucket, tstep, dest, embed_weight, gain, proj_weight, cotangent):
    n_dp = lax.axis_size("dp")
    n_fsdp = lax.axis_size("fsdp")
    myself = lax.axis_index("dp")
    feats = patches.shape[-1]
    width = proj_weight.shape[1]
    total_rows = CAP * TOK_MAX
    length_all = lengths_of(bucket[:, 0])
    dest_col = dest[:, 0]
    source_ids = jnp.arange(n_dp, dtype=jnp.int32)
    my_len = jnp.sum(jnp.where(source_ids == myself, length_all, 0))
    level = noise_level(tstep[0, 0], my_len)
    rows = jnp.arange(TOK_MAX, dtype=jnp.int32)
    mixed = (1.0 - level) * patches[0, 0].astype(jnp.float32) + level * noise[0, 0].astype(
        jnp.float32
    )
    latent = jnp.where(rows[:, None] < my_len, mixed, 0.0).astype(jnp.bfloat16)
    same = dest_col[:, None] == dest_col[None, :]
    earlier = source_ids[None, :] < source_ids[:, None]
    slot = jnp.sum((same & earlier).astype(jnp.int32), axis=1)
    slot_ids = jnp.arange(CAP, dtype=jnp.int32)
    chosen = (dest_col[None, :] == myself) & (slot[None, :] == slot_ids[:, None])
    plen = jnp.sum(jnp.where(chosen, length_all[None, :], 0), axis=1)
    arrived = lax.all_gather(latent[None], "dp", axis=0, tiled=True)
    packed = jnp.dot(
        chosen.astype(jnp.bfloat16),
        arrived.reshape(n_dp, TOK_MAX * feats),
        preferred_element_type=jnp.float32,
    )
    packed = packed.astype(jnp.bfloat16).reshape(total_rows, feats)
    hidden = jnp.dot(packed, embed_weight, preferred_element_type=jnp.float32)
    centered_input = hidden - jnp.mean(hidden, axis=1, keepdims=True)
    inverse_deviation = lax.rsqrt(
        jnp.mean(centered_input * centered_input, axis=1, keepdims=True) + norm_eps
    )
    standardized_input = centered_input * inverse_deviation
    normed_rows = (standardized_input * gain).astype(jnp.bfloat16)
    valid = (rows[None, :] < plen[:, None]).reshape(total_rows, 1)
    cot = cotangent[0, 0].reshape(total_rows, width)
    masked = jnp.where(valid, cot, jnp.zeros_like(cot))
    full_weight = lax.all_gather(proj_weight, "fsdp", axis=0, tiled=True)
    output = jnp.dot(normed_rows, full_weight, preferred_element_type=jnp.float32)
    back = lax.dot_general(
        masked, full_weight, (((1,), (1,)), ((), ())), preferred_element_type=jnp.float32
    )
    input_gradient = back * gain
    hidden_gradient = (
        input_gradient
        - jnp.mean(input_gradient, axis=1, keepdims=True)
        - standardized_input * jnp.mean(input_gradient * standardized_input, axis=1, keepdims=True)
    ) * inverse_deviation
    hidden_gradient = hidden_gradient.astype(jnp.bfloat16)
    partial_value = lax.dot_general(
        packed, hidden_gradient, (((0,), (0,)), ((), ())), preferred_element_type=jnp.float32
    )
    total = lax.psum(partial_value, ("dp", "fsdp"))
    embed_grad = total * float(n_dp * n_fsdp * TOK_MAX) ** (-0.5)
    projected = output.astype(jnp.bfloat16).reshape(1, 1, CAP, TOK_MAX, width)
    return (projected, embed_grad)


def solution(mesh):
    placed = (
        P("dp", "fsdp", None, None),
        P("dp", "fsdp", None, None),
        P(None, "fsdp"),
        P("dp", "fsdp"),
        P(None, "fsdp"),
        P(),
        P(),
        P("fsdp", None),
        P("dp", "fsdp", None, None, None),
    )
    return jax.shard_map(
        body,
        mesh=mesh,
        in_specs=placed,
        out_specs=(P("dp", "fsdp", None, None, None), P()),
        check_vma=False,
    )
```

profile of v0, /device:TPU:0, one launch (start us, length us, event | category | flops | bytes accessed | tf_op | source)
XLA Modules:
  0.0 205.2 jit_solution(9802073919326458462)
XLA Ops:
  7.2 0.0 copy-start
  7.2 0.0 all-gather.2.cloned.1.call-start
  7.2 0.7 all-gather.2.cloned.1.call-update
  7.9 0.0 all-reduce.2.cloned.1.call-start
  8.0 1.3 fusion.7
  10.6 0.7 iota_compare_fusion.2
  11.3 0.8 fusion.4
  12.1 32.6 %all_gather.6 = bf16[8,192,64]{1,2,0:T(8,128)(2,1)S(1)} all-gather(bf16[1,192,64]{1,2,0:T(8,128)(2,1)S(1)} %fusion.4), channel_id=1, replica_groups=mesh['dp'=8,'fsdp'=4] {'dp'}, dimensions={0}, use_global_device_ids=true | all-gather | bytes 221184 | tf_op jit(solution)/shard_map/all_gather | solution.py:47
  44.6 0.2 copy.16
  44.9 0.4 reshape.138
  45.2 0.9 convert_reduce_fusion
  46.2 0.7 broadcast_compare_fusion
  46.8 0.2 convolution_convert_fusion
  47.0 0.1 reshape.139
  47.1 0.7 subtract_bitcast_fusion
  47.8 0.1 select_reduce_fusion
  47.9 0.1 iota_compare_fusion.1
  48.0 0.1 lt.52
  48.1 0.7 fusion.10
  48.8 0.0 copy-start.4
  48.9 1.9 copy-done.1
  50.7 0.5 multiply_reduce_fusion.1
  51.2 0.2 bitcast_select_fusion
  51.4 6.9 %all-gather.2.cloned.1.call-done = bf16[2432,1216]{1,0:T(8,128)(2,1)} async-done(((bf16[608,1216]{1,0:T(8,128)(2,1)}), bf16[2432,1216]{1,0:T(8,128)(2,1)}) %all-gather.2.cloned.1.call-update) | async-done | bytes 5914640 | tf_op jit(solution)/shard_map/all_gather | solution.py:64
  58.3 0.0 copy-done.4
  58.3 7.0 %fusion.9 = (f32[384]{0:T(512)S(1)}, f32[384]{0:T(512)S(1)}, f32[384,2432]{1,0:T(8,128)S(1)}) fusion(f32[384]{0:T(512)S(1)} %add_rsqrt_fusion, f32[384,2432]{1,0:T(8,128)} %copy-done.1, f32[384]{0:T(512)S(1)} %broadcast_multiply_fusion.3, f32[2432]{0:T(1024)S(1)} %copy-done.4, bf16[384,1216]{1,0:T(8,128)(2,1)S(1)} %bitcast_select_fusion, ...), kind=kOutput, calls=%fused_computation.33 | convolution fusion | flops 2276817920 | bytes 14335488 | tf_op jit(solution)/shard_map/dot_general | solution.py:66
  65.3 1.9 fusion.3
  67.3 0.0 all-reduce.2.cloned.1.call-update
  67.3 7.4 %convolution_convert_fusion.1 = bf16[384,1216]{0,1:T(8,128)(2,1)S(1)} fusion(bf16[2432,1216]{1,0:T(8,128)(2,1)} %all-gather.2.cloned.1.call-done, f32[384,2432]{1,0:T(8,128)} %copy-done.1, f32[2432]{0:T(1024)S(1)} %copy-done.4, f32[384]{0:T(512)S(1)} %add_rsqrt_fusion, f32[384]{0:T(512)S(1)} %broadcast_multiply_fusion.3), kind=kOutput, calls=%fused_computation.7 | convolution fusion | flops 2275418112 | bytes 10596864 | tf_op jit(solution)/shard_map/dot_general | solution.py:65
  74.7 1.6 copy.17
  76.3 120.1 %all-reduce.2.cloned.1.call-done = f32[64,2432]{1,0:T(8,128)} async-done(((f32[64,2432]{1,0:T(8,128)}), f32[64,2432]{1,0:T(8,128)}) %all-reduce.2.cloned.1.call-update) | async-done | bytes 622608 | tf_op jit(solution)/shard_map/psum | solution.py:79
  196.4 2.0 broadcast_multiply_fusion
  (9 shorter events, 0.0 us)
Async XLA Ops:
  7.2 40.9 %copy-start = (bf16[64,2432]{1,0:T(8,128)(2,1)S(1)}, bf16[64,2432]{1,0:T(8,128)(2,1)}, u32[]{:S(2)}) copy-start(bf16[64,2432]{1,0:T(8,128)(2,1)} %param.14) | copy-start | bytes 933892
  7.2 51.1 %all-gather.2.cloned.1.call-start = ((), (), s32[]{:S(2)}) async-start(), calls=%async_computation | async-start | bytes 7782400 | tf_op jit(solution)/shard_map/all_gather | solution.py:64
  7.9 188.5 %all-reduce.2.cloned.1.call-start = ((), (), s32[]{:S(2)}) async-start(), calls=%async_computation.1 | async-start | bytes 1245184 | tf_op jit(solution)/shard_map/psum | solution.py:79
  48.1 3.1 %copy-start.3 = (bf16[1,1,2,192,1216]{4,3,2,1,0:T(8,128)(2,1)S(1)}, bf16[1,1,2,192,1216]{4,3,2,1,0:T(8,128)(2,1)}, u32[]{:S(2)}) copy-start(bf16[1,1,2,192,1216]{4,3,2,1,0:T(8,128)(2,1)} %param.17) | copy-start | bytes 2801668
  48.8 1.9 copy-start.1
  48.8 9.5 %copy-start.4 = (f32[2432]{0:T(1024)S(1)}, f32[2432]{0:T(1024)}, u32[]{:S(2)}) copy-start(f32[2432]{0:T(1024)} %param.15) | copy-start | bytes 29188
  58.3 7.0 %copy-start.2 = (f32[384,2432]{1,0:T(8,128)S(1)}, f32[384,2432]{1,0:T(8,128)}, u32[]{:S(2)}) copy-start(f32[384,2432]{1,0:T(8,128)} %copy-done.1) | copy-start | bytes 11206660
Sparse Core Ops, SparseCore 0:
  9.5 48.6 all-gather.1
  67.4 128.9 all-reduce.1
where the time goes:
time: 205 us
  waiting for transfers between devices  128 us (62%)
  blocking collectives  32.6 us (16%)
  matrix products  17.3 us (8%)
  between operations  15.5 us (8%)
  other arithmetic  7.85 us (4%)
  local copies, waits for them, and re-layouts  4.31 us (2%)
    psum x1, waiting for transfers between devices, body(): total = lax.psum(partial_value, ('dp', 'fsdp'))  120 us
    all_gather x1, blocking collectives, body(): arrived = lax.all_gather(latent[None], 'dp', axis=0, tiled=True)  32.6 us
    dot_general x1, matrix products, body(): jnp.dot(normed_rows, full_weight, preferred_element_type=jnp.float32)  7.39 us
    dot_general x1, matrix products, body(): lax.dot_general(masked, full_weight, (((1,), (1,)), ((), ())), preferred_...  7.03 us
    all_gather x1, waiting for transfers between devices, body(): full_weight = lax.all_gather(proj_weight, 'fsdp', axis=0, tiled=True)  6.86 us
  transfers between devices with their start and end apart: 2, of which 2 were waited for; matrix products, arithmetic and copies ran while one was open for 8% of the time, Pallas kernels for 0%

commit v1 on v0

--- a/solution.py
+++ b/solution.py
@@ -44,7 +44,9 @@
     slot_ids = jnp.arange(CAP, dtype=jnp.int32)
     chosen = (dest_col[None, :] == myself) & (slot[None, :] == slot_ids[:, None])
     plen = jnp.sum(jnp.where(chosen, length_all[None, :], 0), axis=1)
-    arrived = lax.all_gather(latent[None], "dp", axis=0, tiled=True)
+    arrived = jnp.concatenate(
+        lax.all_to_all(jnp.stack([latent[None]] * lax.axis_size("dp")), "dp", 0, 0), axis=0
+    )
     packed = jnp.dot(
         chosen.astype(jnp.bfloat16),
         arrived.reshape(n_dp, TOK_MAX * feats),

time: 205 us -> 206 us (level)
  blocking collectives: 32.6 us -> 0 us
  waiting for transfers between devices: 128 us -> 151 us
  starting transfers between devices: 0.08 us -> 7.36 us
    all_gather x1 -> x0, blocking collectives: 32.6 us -> none  [body(): arrived = lax.all_gather(latent[None], 'dp', axis=0, tiled=True)]
    all_gather x1, waiting for transfers between devices: 6.86 us -> 25.3 us  [body(): full_weight = lax.all_gather(proj_weight, 'fsdp', axis=0, tiled=True)]
    all_to_all x0 -> x1, starting transfers between devices: none -> 7.28 us  [body(): lax.all_to_all(jnp.stack([latent[None]] * lax.axis_size('dp')), 'dp', 0, 0)]
    all_to_all x0 -> x1, waiting for transfers between devices: none -> 4.91 us  [body(): lax.all_to_all(jnp.stack([latent[None]] * lax.axis_size('dp')), 'dp', 0, 0)]
  transfers between devices with their start and end apart: 2 -> 3, of which waited for: 2 -> 3; matrix products, arithmetic and copies ran while one was open for 8% -> 9% of each run, Pallas kernels for 0% -> 0%
where the time goes in v1:
time: 206 us; the launch traced here: 205 us
  waiting for transfers between devices  151 us (73%)
  matrix products  17.3 us (8%)
  between operations  15.5 us (8%)
  other arithmetic  9.09 us (4%)
  starting transfers between devices  7.36 us (4%)
  local copies, waits for them, and re-layouts  5.02 us (2%)
    psum x1, waiting for transfers between devices, body(): total = lax.psum(partial_value, ('dp', 'fsdp'))  120 us
    all_gather x1, waiting for transfers between devices, body(): full_weight = lax.all_gather(proj_weight, 'fsdp', axis=0, tiled=True)  25.3 us
    dot_general x1, matrix products, body(): jnp.dot(normed_rows, full_weight, preferred_element_type=jnp.float32)  7.38 us
    all_to_all x1, starting transfers between devices, body(): lax.all_to_all(jnp.stack([latent[None]] * lax.axis_size('dp')), 'dp', 0, 0)  7.28 us
    dot_general x1, matrix products, body(): lax.dot_general(masked, full_weight, (((1,), (1,)), ((), ())), preferred_...  7.04 us
    all_to_all x1, waiting for transfers between devices, body(): lax.all_to_all(jnp.stack([latent[None]] * lax.axis_size('dp')), 'dp', 0, 0)  4.91 us
  transfers between devices with their start and end apart: 3, of which 3 were waited for; matrix products, arithmetic and copies ran while one was open for 9% of the time, Pallas kernels for 0%

profile of v1, /device:TPU:0, one launch (start us, length us, event | category | flops | bytes accessed | tf_op | source)
XLA Modules:
  0.0 205.2 jit_solution(17258590425931834537)
XLA Ops:
  7.2 0.0 copy-start
  7.2 0.0 all-gather.2.cloned.1.call-start
  7.2 0.7 all-gather.2.cloned.1.call-update
  7.9 1.3 fusion.7
  10.6 0.7 iota_compare_fusion.2
  11.2 0.8 fusion.4
  12.0 0.7 stack.3
  12.7 7.3 %all-to-all-start = ((bf16[8,1,192,64]{2,3,1,0:T(8,128)(2,1)}), bf16[8,1,192,64]{2,3,1,0:T(8,128)(2,1)S(1)}, u32[]{:S(2)}, u32[]{:S(2)}) async-start(bf16[8,1,192,64]{2,3,1,0:T(8,128)(2,1)} %stack.3), calls=%async_computation | async-start | bytes 524288 | tf_op jit(solution)/shard_map/all_to_all | solution.py:48
  20.0 0.0 all-reduce.2.cloned.1.call-start
  20.1 0.9 convert_reduce_fusion
  21.0 0.7 broadcast_compare_fusion
  21.6 0.7 subtract_bitcast_fusion
  22.3 0.1 select_reduce_fusion
  22.4 0.1 iota_compare_fusion.1
  22.5 0.1 lt.52
  22.6 1.4 bitcast_select_fusion
  24.0 4.9 %all-to-all-done = bf16[8,1,192,64]{2,3,1,0:T(8,128)(2,1)S(1)} async-done(((bf16[8,1,192,64]{2,3,1,0:T(8,128)(2,1)}), bf16[8,1,192,64]{2,3,1,0:T(8,128)(2,1)S(1)}, u32[]{:S(2)}, u32[]{:S(2)}) %all-to-all-start) | async-done | bytes 196640 | tf_op jit(solution)/shard_map/all_to_all | solution.py:48
  28.9 0.2 copy.17
  29.2 0.4 reshape_reshape.3
  29.5 0.2 convolution_convert_fusion
  29.7 0.1 reshape.84
  29.9 0.7 fusion.10
  30.6 1.9 copy-done.1
  32.5 0.5 multiply_reduce_fusion.1
  33.0 25.3 %all-gather.2.cloned.1.call-done = bf16[2432,1216]{1,0:T(8,128)(2,1)} async-done(((bf16[608,1216]{1,0:T(8,128)(2,1)}), bf16[2432,1216]{1,0:T(8,128)(2,1)}) %all-gather.2.cloned.1.call-update) | async-done | bytes 5914640 | tf_op jit(solution)/shard_map/all_gather | solution.py:66
  58.3 7.0 %fusion.9 = (f32[384]{0:T(512)S(1)}, f32[384]{0:T(512)S(1)}, f32[384,2432]{1,0:T(8,128)S(1)}) fusion(f32[384]{0:T(512)S(1)} %add_rsqrt_fusion, f32[384,2432]{1,0:T(8,128)} %copy-done.1, f32[384]{0:T(512)S(1)} %broadcast_multiply_fusion.3, f32[2432]{0:T(1024)S(1)} %copy-done.3, bf16[384,1216]{1,0:T(8,128)(2,1)S(1)} %bitcast_select_fusion, ...), kind=kOutput, calls=%fused_computation.33 | convolution fusion | flops 2276817920 | bytes 14335488 | tf_op jit(solution)/shard_map/dot_general | solution.py:68
  65.4 1.9 fusion.3
  67.3 0.0 all-reduce.2.cloned.1.call-update
  67.3 7.4 %convolution_convert_fusion.1 = bf16[384,1216]{0,1:T(8,128)(2,1)S(1)} fusion(bf16[2432,1216]{1,0:T(8,128)(2,1)} %all-gather.2.cloned.1.call-done, f32[384,2432]{1,0:T(8,128)} %copy-done.1, f32[2432]{0:T(1024)S(1)} %copy-done.3, f32[384]{0:T(512)S(1)} %add_rsqrt_fusion, f32[384]{0:T(512)S(1)} %broadcast_multiply_fusion.3), kind=kOutput, calls=%fused_computation.7 | convolution fusion | flops 2275418112 | bytes 10596864 | tf_op jit(solution)/shard_map/dot_general | solution.py:67
  74.7 1.6 copy.18
  76.3 120.0 %all-reduce.2.cloned.1.call-done = f32[64,2432]{1,0:T(8,128)} async-done(((f32[64,2432]{1,0:T(8,128)}), f32[64,2432]{1,0:T(8,128)}) %all-reduce.2.cloned.1.call-update) | async-done | bytes 622608 | tf_op jit(solution)/shard_map/psum | solution.py:81
  196.4 2.0 broadcast_multiply_fusion
  (9 shorter events, 0.0 us)
Async XLA Ops:
  7.2 22.7 %copy-start = (bf16[64,2432]{1,0:T(8,128)(2,1)S(1)}, bf16[64,2432]{1,0:T(8,128)(2,1)}, u32[]{:S(2)}) copy-start(bf16[64,2432]{1,0:T(8,128)(2,1)} %param.14) | copy-start | bytes 933892
  7.2 51.1 %all-gather.2.cloned.1.call-start = ((), (), s32[]{:S(2)}) async-start(), calls=%async_computation.1 | async-start | bytes 7782400 | tf_op jit(solution)/shard_map/all_gather | solution.py:66
  12.7 16.2 %all-to-all-start = ((bf16[8,1,192,64]{2,3,1,0:T(8,128)(2,1)}), bf16[8,1,192,64]{2,3,1,0:T(8,128)(2,1)S(1)}, u32[]{:S(2)}, u32[]{:S(2)}) async-start(bf16[8,1,192,64]{2,3,1,0:T(8,128)(2,1)} %stack.3), calls=%async_computation | async-start | bytes 524288 | tf_op jit(solution)/shard_map/all_to_all | solution.py:48
  20.0 176.3 %all-reduce.2.cloned.1.call-start = ((), (), s32[]{:S(2)}) async-start(), calls=%async_computation.2 | async-start | bytes 1245184 | tf_op jit(solution)/shard_map/psum | solution.py:81
  29.9 28.4 %copy-start.3 = (f32[2432]{0:T(1024)S(1)}, f32[2432]{0:T(1024)}, u32[]{:S(2)}) copy-start(f32[2432]{0:T(1024)} %param.15) | copy-start | bytes 29188
  30.6 1.9 copy-start.1
  58.3 7.1 %copy-start.2 = (f32[384,2432]{1,0:T(8,128)S(1)}, f32[384,2432]{1,0:T(8,128)}, u32[]{:S(2)}) copy-start(f32[384,2432]{1,0:T(8,128)} %copy-done.1) | copy-start | bytes 11206660
Sparse Core Ops, SparseCore 0:
  9.5 48.6 all-gather.1
  67.4 128.8 all-reduce.1

commit v2 on v0

--- a/solution.py
+++ b/solution.py
@@ -76,7 +76,7 @@
     partial_value = lax.dot_general(
         packed, hidden_gradient, (((0,), (0,)), ((), ())), preferred_element_type=jnp.float32
     )
-    total = lax.psum(partial_value, ("dp", "fsdp"))
+    total = jnp.sum(lax.all_gather(partial_value, ("dp", "fsdp")), axis=0)
     embed_grad = total * float(n_dp * n_fsdp * TOK_MAX) ** (-0.5)
     projected = output.astype(jnp.bfloat16).reshape(1, 1, CAP, TOK_MAX, width)
     return (projected, embed_grad)

time: 205 us -> 212 us (1.034)
  other arithmetic: 7.85 us -> 14.4 us
    psum x1 -> x0, waiting for transfers between devices: 120 us -> none  [body(): total = lax.psum(partial_value, ('dp', 'fsdp'))]
    all_gather x0 -> x1, waiting for transfers between devices: none -> 120 us  [body(): total = jnp.sum(lax.all_gather(partial_value, ('dp', 'fsdp')), axis=0)]
    reduce_sum x0 -> x1, other arithmetic: none -> 7.61 us  [body(): total = jnp.sum(lax.all_gather(partial_value, ('dp', 'fsdp')), axis=0)]
where the time goes in v2:
time: 212 us
  waiting for transfers between devices  128 us (60%)
  blocking collectives  32.6 us (15%)
  matrix products  17.3 us (8%)
  between operations  15.5 us (7%)
  other arithmetic  14.4 us (7%)
  local copies, waits for them, and re-layouts  4.26 us (2%)
    all_gather x1, waiting for transfers between devices, body(): total = jnp.sum(lax.all_gather(partial_value, ('dp', 'fsdp')), axis=0)  120 us
    all_gather x1, blocking collectives, body(): arrived = lax.all_gather(latent[None], 'dp', axis=0, tiled=True)  32.6 us
    reduce_sum x1, other arithmetic, body(): total = jnp.sum(lax.all_gather(partial_value, ('dp', 'fsdp')), axis=0)  7.61 us
    dot_general x1, matrix products, body(): jnp.dot(normed_rows, full_weight, preferred_element_type=jnp.float32)  7.39 us
    dot_general x1, matrix products, body(): lax.dot_general(masked, full_weight, (((1,), (1,)), ((), ())), preferred_...  7.03 us
    all_gather x1, waiting for transfers between devices, body(): full_weight = lax.all_gather(proj_weight, 'fsdp', axis=0, tiled=True)  6.9 us
  transfers between devices with their start and end apart: 2, of which 2 were waited for; matrix products, arithmetic and copies ran while one was open for 8% of the time, Pallas kernels for 0%

profile of v2, /device:TPU:0, one launch (start us, length us, event | category | flops | bytes accessed | tf_op | source)
XLA Modules:
  0.0 211.6 jit_solution(9415582434971725802)
XLA Ops:
  7.2 0.0 copy-start
  7.2 0.0 all-gather.4.cloned.1.call-start
  7.2 0.7 all-gather.4.cloned.1.call-update
  7.9 0.0 all-gather.6.cloned.1.call-start
  8.6 1.3 fusion.7
  10.6 0.9 convert_reduce_fusion
  11.5 0.7 broadcast_compare_fusion
  12.2 0.7 subtract_bitcast_fusion
  12.8 0.1 select_reduce_fusion
  13.0 0.1 iota_compare_fusion.1
  13.0 0.1 lt.52
  13.1 0.7 iota_compare_fusion.2
  13.8 0.8 fusion.4
  14.6 32.6 %all_gather.12 = bf16[8,192,64]{1,2,0:T(8,128)(2,1)S(1)} all-gather(bf16[1,192,64]{1,2,0:T(8,128)(2,1)S(1)} %fusion.4), channel_id=1, replica_groups=mesh['dp'=8,'fsdp'=4] {'dp'}, dimensions={0}, use_global_device_ids=true | all-gather | bytes 221184 | tf_op jit(solution)/shard_map/all_gather | solution.py:47
  47.1 0.2 copy.16
  47.4 0.4 reshape.138
  47.7 0.2 convolution_convert_fusion
  47.9 0.1 reshape.139
  48.1 0.0 copy-start.3
  48.1 0.7 fusion.10
  48.8 1.8 copy-done.1
  50.7 0.5 multiply_reduce_fusion.1
  51.2 0.2 bitcast_select_fusion
  51.4 6.9 %all-gather.4.cloned.1.call-done = bf16[2432,1216]{1,0:T(8,128)(2,1)} async-done(((bf16[608,1216]{1,0:T(8,128)(2,1)}), bf16[2432,1216]{1,0:T(8,128)(2,1)}) %all-gather.4.cloned.1.call-update) | async-done | bytes 5914640 | tf_op jit(solution)/shard_map/all_gather | solution.py:64
  58.3 7.0 %fusion.9 = (f32[384]{0:T(512)S(1)}, f32[384]{0:T(512)S(1)}, f32[384,2432]{1,0:T(8,128)S(1)}) fusion(f32[384]{0:T(512)S(1)} %add_rsqrt_fusion, f32[384,2432]{1,0:T(8,128)} %copy-done.1, f32[384]{0:T(512)S(1)} %broadcast_multiply_fusion.3, f32[2432]{0:T(1024)S(1)} %copy-done.4, bf16[384,1216]{1,0:T(8,128)(2,1)S(1)} %bitcast_select_fusion, ...), kind=kOutput, calls=%fused_computation.33 | convolution fusion | flops 2276817920 | bytes 14335488 | tf_op jit(solution)/shard_map/dot_general | solution.py:66
  65.4 1.9 fusion.3
  67.3 0.0 all-gather.6.cloned.1.call-update
  67.3 7.4 %convolution_convert_fusion.1 = bf16[384,1216]{0,1:T(8,128)(2,1)S(1)} fusion(bf16[2432,1216]{1,0:T(8,128)(2,1)} %all-gather.4.cloned.1.call-done, f32[384,2432]{1,0:T(8,128)} %copy-done.1, f32[2432]{0:T(1024)S(1)} %copy-done.4, f32[384]{0:T(512)S(1)} %add_rsqrt_fusion, f32[384]{0:T(512)S(1)} %broadcast_multiply_fusion.3), kind=kOutput, calls=%fused_computation.7 | convolution fusion | flops 2275418112 | bytes 10596864 | tf_op jit(solution)/shard_map/dot_general | solution.py:65
  74.7 1.6 copy.17
  76.3 120.0 %all-gather.6.cloned.1.call-done = f32[2048,2432]{1,0:T(8,128)} async-done(((f32[64,2432]{1,0:T(8,128)}), f32[2048,2432]{1,0:T(8,128)}) %all-gather.6.cloned.1.call-update) | async-done | bytes 19922960 | tf_op jit(solution)/shard_map/all_gather | solution.py:79
  196.3 7.6 %reduce_sum.79 = f32[64,2432]{1,0:T(8,128)S(1)} reduce(f32[32,64,2432]{2,1,0:T(8,128)} %bitcast.22, f32[]{:T(128)} %constant.37.clone.1), dimensions={0}, to_apply=%region_7.8 | reduce | flops 4825088 | bytes 20545540 | tf_op jit(solution)/shard_map/reduce_sum | solution.py:79
  203.9 0.9 broadcast_multiply_fusion
  (10 shorter events, 0.0 us)
Async XLA Ops:
  7.2 40.9 %copy-start = (bf16[64,2432]{1,0:T(8,128)(2,1)S(1)}, bf16[64,2432]{1,0:T(8,128)(2,1)}, u32[]{:S(2)}) copy-start(bf16[64,2432]{1,0:T(8,128)(2,1)} %param.14) | copy-start | bytes 933892
  7.2 51.1 %all-gather.4.cloned.1.call-start = ((), (), s32[]{:S(2)}) async-start(), calls=%async_computation | async-start | bytes 7782400 | tf_op jit(solution)/shard_map/all_gather | solution.py:64
  7.9 188.4 %all-gather.6.cloned.1.call-start = ((), (), s32[]{:S(2)}) async-start(), calls=%async_computation.1 | async-start | bytes 20545536 | tf_op jit(solution)/shard_map/all_gather | solution.py:79
  48.1 3.1 %copy-start.3 = (bf16[1,1,2,192,1216]{4,3,2,1,0:T(8,128)(2,1)S(1)}, bf16[1,1,2,192,1216]{4,3,2,1,0:T(8,128)(2,1)}, u32[]{:S(2)}) copy-start(bf16[1,1,2,192,1216]{4,3,2,1,0:T(8,128)(2,1)} %param.17) | copy-start | bytes 2801668
  48.8 1.9 copy-start.1
  48.8 9.5 %copy-start.4 = (f32[2432]{0:T(1024)S(1)}, f32[2432]{0:T(1024)}, u32[]{:S(2)}) copy-start(f32[2432]{0:T(1024)} %param.15) | copy-start | bytes 29188
  58.3 7.0 %copy-start.2 = (f32[384,2432]{1,0:T(8,128)S(1)}, f32[384,2432]{1,0:T(8,128)}, u32[]{:S(2)}) copy-start(f32[384,2432]{1,0:T(8,128)} %copy-done.1) | copy-start | bytes 11206660
Sparse Core Ops, SparseCore 0:
  9.5 48.6 all-gather.3
  67.4 128.8 all-gather.5
